TPU v7x, 32 devices: a whole 2x2x4 slice. The times are simulated.
32 devices in a mesh: rep: 2 (over y), own: 16 (over z, x, core).
Axes of the slice: x: 2, y: 2, z: 4, core: 2. Of those that a mesh axis runs over, the one named last changes fastest.
Arguments:
- values: float32 [262144, 128], P(('rep', 'own')), may hold values from -0.8 to 0.8
- key_ids: int32 [262144], P(('rep', 'own')), may hold values from 0 to 65535, as said below
- heavy_ids: int32 [2048], replicated, may hold values from 0 to 65535, as said below
- block_offsets: int32 [32, 16], P(('rep', 'own')), may hold values from 0 to 8191, as said below
- block_counts: int32 [32, 16], P(('rep', 'own')), may hold values from 8 to 64, as said below
Outputs:
- light_sums: float32 [65536, 128], P('own')
- heavy_sums: float32 [2048, 128], P('own')
Inputs may be any that keep to these rules, and one draw needn't show every extreme that they name: `key_ids`: an event in block o of a device has a key in o * 4096 to (o + 1) * 4096 - 1 that is not a heavy key; every event outside all blocks has a heavy key. `heavy_ids`: distinct keys. `block_offsets`: on each device the blocks lie in the order of o, do not meet, and end by position 8192. `block_counts`: at most 64; one owner gets exactly 64 from every device.
All inputs are finite; a program needn't handle non-finite values.
Results may differ from a plain program's by a relative error of at most 0.000075.
Values sent between devices are 32-bit elements; how exact they have to be, the bound alone decides.
A program may use at most 64 MiB of HBM per device.

v0:
```python
import math
import jax
import jax.numpy as jnp
from jax import lax
from jax.sharding import PartitionSpec as P

KEYS_DEV = 4096
CAP = 64


def key_sums(rows_in, row_keys, targets):
    slots = row_keys.shape[0]
    block_len = math.gcd(slots, 2048)
    count_blocks = slots // block_len
    rows_blocks = rows_in.reshape(count_blocks, block_len, rows_in.shape[1])
    keys_blocks = row_keys.reshape(count_blocks, block_len)

    def accumulate(running, pieces):
        rows_piece, keys_piece = pieces
        onehot = (targets[:, None] == keys_piece[None, :]).astype(jnp.float32)
        added = jnp.dot(
            onehot, rows_piece, precision=lax.Precision.HIGHEST, preferred_element_type=jnp.float32
        )
        return (running + added, None)

    start_sums = jnp.zeros((targets.shape[0], rows_in.shape[1]), jnp.float32)
    running, unused = lax.scan(accumulate, start_sums, (rows_blocks, keys_blocks))
    return running


def per_device(values, key_ids, heavy_ids, block_offsets, block_counts):
    owners = lax.axis_size("own")
    pairs = lax.axis_size("rep")
    own_index = lax.axis_index("own")
    rep_index = lax.axis_index("rep")
    width = values.shape[1]
    slot_cap = CAP
    padded_values = jnp.concatenate([values, jnp.zeros((slot_cap, width), jnp.float32)], axis=0)
    padded_keys = jnp.concatenate([key_ids, jnp.full((slot_cap,), -1, jnp.int32)], axis=0)
    slot_iota = jnp.arange(slot_cap, dtype=jnp.int32)
    positions = block_offsets[0][:, None] + slot_iota[None, :]
    valid = slot_iota[None, :] < block_counts[0][:, None]
    block_rows = jnp.where(valid[:, :, None], jnp.take(padded_values, positions, axis=0), 0.0)
    block_keys = jnp.where(valid, jnp.take(padded_keys, positions, axis=0), -1)
    half_keys = KEYS_DEV // 2
    owner_base = (jnp.arange(owners, dtype=jnp.int32) * KEYS_DEV)[:, None]
    which_half = jnp.where(block_keys >= 0, (block_keys - owner_base) // half_keys, -1)
    split_rows = jnp.stack(
        [jnp.where((which_half == side)[:, :, None], block_rows, 0.0) for side in range(pairs)],
        axis=0,
    )
    split_keys = jnp.stack(
        [jnp.where(which_half == side, block_keys, -1) for side in range(pairs)], axis=0
    )
    split_rows = split_rows.reshape(pairs * owners, slot_cap, width)
    split_keys = split_keys.reshape(pairs * owners, slot_cap)
    got_rows, got_keys = (
        lax.all_to_all(split_rows, ("rep", "own"), split_axis=0, concat_axis=0, tiled=True),
        lax.all_to_all(split_keys, ("rep", "own"), split_axis=0, concat_axis=0, tiled=True),
    )
    local_keys = jnp.where(
        got_keys >= 0, got_keys - own_index * KEYS_DEV - rep_index * half_keys, -1
    ).reshape(-1)
    owned_half = key_sums(
        got_rows.reshape(-1, width), local_keys, jnp.arange(half_keys, dtype=jnp.int32)
    )
    light_sums = lax.all_gather(owned_half, "rep", axis=0, tiled=True)
    partial_sums = key_sums(values, key_ids, heavy_ids)
    summed_pair = lax.psum(partial_sums, "rep")
    heavy_sums = lax.psum_scatter(summed_pair, "own", scatter_dimension=0, tiled=True)
    return (light_sums, heavy_sums)


def solution(mesh):
    placed = (
        P(("rep", "own"), None),
        P(("rep", "own")),
        P(),
        P(("rep", "own"), None),
        P(("rep", "own"), None),
    )
    return jax.shard_map(
        per_device,
        mesh=mesh,
        in_specs=placed,
        out_specs=(P("own", None), P("own", None)),
        check_vma=False,
    )
```

profile of v0, /device:TPU:0, one launch (start us, length us, event | category | flops | bytes accessed | tf_op | source)
XLA Modules:
  0.0 166.0 jit_solution(6468750620577032743)
XLA Ops:
  8.0 0.7 compare_select_fusion.2
  8.7 0.1 reshape.548
  8.8 0.8 concatenate.6
  9.6 0.0 copy-start.3
  9.6 0.0 copy-start.4
  9.6 6.1 %gather_fusion = s32[1024]{0:T(1024)S(1)} fusion(s32[8256]{0:T(1024)S(1)} %concatenate.6, s32[1024]{0:T(1024)S(1)} %broadcast_clamp_fusion), kind=kCustom, calls=%fused_computation | custom fusion | bytes 12288 | tf_op jit(solution)/shard_map/jit(_take)/gather | solution.py:44
  15.7 0.1 gather.13
  15.8 0.0 copy-done.3
  15.8 0.0 copy-done.4
  15.8 0.1 compare_select_fusion.5
  15.9 0.6 pad_add_fusion
  16.5 7.3 %all-to-all-start = ((s32[32,1,64]{2,1,0:T(1,128)}), s32[32,1,64]{2,1,0:T(1,128)S(1)}, u32[]{:S(2)}, u32[]{:S(2)}) async-start(s32[32,1,64]{2,1,0:T(1,128)} %bitcast.2), calls=%async_computation | async-start | bytes 32768 | tf_op jit(solution)/shard_map/all_to_all | solution.py:59
  23.8 0.1 reshape.547
  23.9 3.7 %concatenate.7 = f32[8256,128]{1,0:T(8,128)} pad(f32[8192,128]{1,0:T(8,128)} %param.7, f32[]{:T(128)} %constant.82.clone.1), padding=0_64x0_0 | pad | bytes 8421380 | tf_op jit(solution)/shard_map/concatenate | solution.py:38
  27.6 0.0 copy-start.1
  27.6 0.0 copy-start.5
  27.6 5.0 %gather_fusion.1 = f32[1024,128]{1,0:T(8,128)S(1)} fusion(f32[8256,128]{1,0:T(8,128)} %concatenate.7, s32[1024]{0:T(1024)S(1)} %broadcast_clamp_fusion), kind=kCustom, calls=%fused_computation.1 | custom fusion | bytes 1052672 | tf_op jit(solution)/shard_map/jit(_take)/gather | solution.py:43
  32.6 0.1 broadcast_compare_fusion.1
  32.8 0.7 fusion.13
  33.5 1.1 pad_maximum_fusion
  34.6 0.0 copy-done.1
  34.6 0.0 all-to-all-done
  34.6 5.8 %all-to-all-start.1 = ((f32[32,64,128]{2,1,0:T(8,128)}), f32[32,64,128]{2,1,0:T(8,128)S(1)}, u32[]{:S(2)}, u32[]{:S(2)}) async-start(f32[32,64,128]{2,1,0:T(8,128)} %bitcast.4), calls=%async_computation.1 | async-start | bytes 2097152 | tf_op jit(solution)/shard_map/all_to_all | solution.py:58
  40.4 0.0 reduce-scatter.2.cloned.1.call-start
  40.5 0.0 copy-done.5
  40.5 34.5 %while.3 = (s32[]{:T(128)}, f32[2048,128]{1,0:T(8,128)S(1)}, s32[2048]{0:T(1024)S(1)}, s32[4,2048]{1,0:T(4,128)S(1)}, f32[4,2048,128]{2,1,0:T(8,128)}, /*index=5*/s32[]{:T(128)}, s32[]{:T(128)}) while((s32[]{:T(128)}, f32[2048,128]{1,0:T(8,128)S(1)}, s32[2048]{0:T(1024)S(1)}, s32[4,2048]{1,0:T(4,128)S(1)}, ...), condition=%wide.region_1.2_spmd.clone, body=%wide.region_0.1_spmd.clone.sunk | while | flops 6447169536 | bytes 3178599 | solution.py:27
  40.5 8.6 %fusion.34 = f32[2048,128]{1,0:T(8,128)S(1)} fusion(s32[2048]{0:T(1024)S(1)} %bitcast.21, s32[2048]{0:T(1024)S(1)} %get-tuple-element.128, f32[2048,128]{1,0:T(8,128)S(1)} %get-tuple-element.120, f32[4,2048,128]{2,1,0:T(8,128)} %get-tuple-element.130, s32[]{:T(128)S(6)} %copy.9, pred[]{:T(512)S(6)} %compare.29), kind=kOutput, calls=%fused_computation.6.clone.1 | convolution fusion | flops 6447169536 | bytes 3162117 | tf_op jit(solution)/shard_map/while/body/eval_jaxpr/dot_general | solution.py:21
  49.2 8.6 %fusion.34 = f32[2048,128]{1,0:T(8,128)S(1)} fusion(s32[2048]{0:T(1024)S(1)} %bitcast.21, s32[2048]{0:T(1024)S(1)} %get-tuple-element.128, f32[2048,128]{1,0:T(8,128)S(1)} %get-tuple-element.120, f32[4,2048,128]{2,1,0:T(8,128)} %get-tuple-element.130, s32[]{:T(128)S(6)} %copy.9, pred[]{:T(512)S(6)} %compare.29), kind=kOutput, calls=%fused_computation.6.clone.1 | convolution fusion | flops 6447169536 | bytes 3162117 | tf_op jit(solution)/shard_map/while/body/eval_jaxpr/dot_general | solution.py:21
  57.8 8.6 %fusion.34 = f32[2048,128]{1,0:T(8,128)S(1)} fusion(s32[2048]{0:T(1024)S(1)} %bitcast.21, s32[2048]{0:T(1024)S(1)} %get-tuple-element.128, f32[2048,128]{1,0:T(8,128)S(1)} %get-tuple-element.120, f32[4,2048,128]{2,1,0:T(8,128)} %get-tuple-element.130, s32[]{:T(128)S(6)} %copy.9, pred[]{:T(512)S(6)} %compare.29), kind=kOutput, calls=%fused_computation.6.clone.1 | convolution fusion | flops 6447169536 | bytes 3162117 | tf_op jit(solution)/shard_map/while/body/eval_jaxpr/dot_general | solution.py:21
  66.4 8.6 %fusion.34 = f32[2048,128]{1,0:T(8,128)S(1)} fusion(s32[2048]{0:T(1024)S(1)} %bitcast.21, s32[2048]{0:T(1024)S(1)} %get-tuple-element.128, f32[2048,128]{1,0:T(8,128)S(1)} %get-tuple-element.120, f32[4,2048,128]{2,1,0:T(8,128)} %get-tuple-element.130, s32[]{:T(128)S(6)} %copy.9, pred[]{:T(512)S(6)} %compare.29), kind=kOutput, calls=%fused_computation.6.clone.1 | convolution fusion | flops 6447169536 | bytes 3162117 | tf_op jit(solution)/shard_map/while/body/eval_jaxpr/dot_general | solution.py:21
  75.0 0.0 copy-start
  75.0 1.0 copy-done
  76.0 0.0 reduce-scatter.2.cloned.1.call-update
  76.0 0.2 all-gather.2.cloned.1.call-start
  76.2 0.1 fusion.14
  76.3 0.1 select_n.222
  76.4 0.0 all-to-all-done.1
  76.4 8.6 %fusion.10 = f32[2048,128]{1,0:T(8,128)} fusion(f32[2048,128]{1,0:T(8,128)S(1)} %bitcast.20, s32[2048]{0:T(1024)S(1)} %select_n.222), kind=kOutput, calls=%fused_computation.12 | convolution fusion | flops 6446645248 | bytes 2105344 | tf_op jit(solution)/shard_map/while/body/eval_jaxpr/dot_general | solution.py:21
  84.9 0.0 all-gather.2.cloned.1.call-update
  85.0 0.0 all-reduce.4.cloned.1.call-start
  85.0 50.0 %reduce-scatter.2.cloned.1.call-done = f32[128,128]{1,0:T(8,128)} async-done(((f32[2048,128]{1,0:T(8,128)}), f32[128,128]{1,0:T(8,128)}) %reduce-scatter.2.cloned.1.call-update) | async-done | bytes 65552 | tf_op jit(solution)/shard_map/reduce_scatter | solution.py:70
  135.0 0.0 all-reduce.4.cloned.1.call-update
  135.0 0.0 all-gather.2.cloned.1.call-done
  135.0 19.8 %all-reduce.4.cloned.1.call-done = f32[128,128]{1,0:T(8,128)} async-done(((f32[128,128]{1,0:T(8,128)}), f32[128,128]{1,0:T(8,128)}) %all-reduce.4.cloned.1.call-update) | async-done | bytes 65552 | tf_op jit(solution)/shard_map/psum | solution.py:69
  154.9 0.0 copy-start.2
  154.9 3.1 %copy.15 = f32[4096,128]{1,0:T(8,128)} copy(f32[4096,128]{1,0:T(8,128)} %all-gather.2.cloned.1.call-done) | data formatting | bytes 4194304
  157.9 0.0 copy-done.2
  157.9 0.6 copy.16
  (9 shorter events, 0.1 us)
Async XLA Ops:
  9.6 6.2 %copy-start.3 = (s32[1,16]{1,0:T(1,128)S(1)}, s32[1,16]{1,0:T(1,128)}, u32[]{:S(2)}) copy-start(s32[1,16]{1,0:T(1,128)} %param.10) | copy-start | bytes 196
  9.6 6.2 %copy-start.4 = (s32[1,16]{1,0:T(1,128)S(1)}, s32[1,16]{1,0:T(1,128)}, u32[]{:S(2)}) copy-start(s32[1,16]{1,0:T(1,128)} %param.11) | copy-start | bytes 196
  16.5 18.1 %all-to-all-start = ((s32[32,1,64]{2,1,0:T(1,128)}), s32[32,1,64]{2,1,0:T(1,128)S(1)}, u32[]{:S(2)}, u32[]{:S(2)}) async-start(s32[32,1,64]{2,1,0:T(1,128)} %bitcast.2), calls=%async_computation | async-start | bytes 32768 | tf_op jit(solution)/shard_map/all_to_all | solution.py:59
  27.6 6.9 %copy-start.1 = (s32[8192]{0:T(1024)S(1)}, s32[8192]{0:T(1024)}, u32[]{:S(2)}) copy-start(s32[8192]{0:T(1024)} %param.8) | copy-start | bytes 98308
  27.6 12.9 %copy-start.5 = (s32[2048]{0:T(1024)S(1)}, s32[2048]{0:T(1024)}, u32[]{:S(2)}) copy-start(s32[2048]{0:T(1024)} %param.9) | copy-start | bytes 24580
  34.6 41.8 %all-to-all-start.1 = ((f32[32,64,128]{2,1,0:T(8,128)}), f32[32,64,128]{2,1,0:T(8,128)S(1)}, u32[]{:S(2)}, u32[]{:S(2)}) async-start(f32[32,64,128]{2,1,0:T(8,128)} %bitcast.4), calls=%async_computation.1 | async-start | bytes 2097152 | tf_op jit(solution)/shard_map/all_to_all | solution.py:58
  40.4 94.5 %reduce-scatter.2.cloned.1.call-start = ((), (), s32[]{:S(2)}) async-start(), calls=%async_computation.4 | async-start | bytes 1114112 | tf_op jit(solution)/shard_map/reduce_scatter | solution.py:70
  75.0 1.0 copy-start
  76.0 59.1 %all-gather.2.cloned.1.call-start = ((), (), s32[]{:S(2)}) async-start(), calls=%async_computation.3 | async-start | bytes 3145728 | tf_op jit(solution)/shard_map/all_gather | solution.py:67
  85.0 69.9 %all-reduce.4.cloned.1.call-start = ((), (), s32[]{:S(2)}) async-start(), calls=%async_computation.5 | async-start | bytes 131072 | tf_op jit(solution)/shard_map/psum | solution.py:69
  154.9 3.1 %copy-start.2 = (f32[128,128]{1,0:T(8,128)S(1)}, f32[128,128]{1,0:T(8,128)}, u32[]{:S(2)}) copy-start(f32[128,128]{1,0:T(8,128)} %all-reduce.4.cloned.1.call-done) | copy-start | bytes 196612
Sparse Core Ops, SparseCore 0:
  76.1 58.8 reduce-scatter.1
Sparse Core Ops, SparseCore 1:
  85.0 34.2 all-gather.1
  135.1 19.7 all-reduce.3
where the time goes:
time: 167 us; the launch traced here: 166 us
  waiting for transfers between devices  69.9 us (42%)
  matrix products  42.9 us (26%)
  local copies, waits for them, and re-layouts  20.7 us (12%)
  between operations  15.6 us (9%)
  starting transfers between devices  13.5 us (8%)
  other arithmetic  3.39 us (2%)
    reduce_scatter x1, waiting for transfers between devices, per_device(): lax.psum_scatter(summed_pair, 'own', scatter_dimension=0, tiled=True)  50 us
    dot_general x5, matrix products, accumulate(): jnp.dot(onehot, rows_piece, precision=lax.Precision.HIGHEST, preferred_el...  42.9 us
    psum x1, waiting for transfers between devices, per_device(): summed_pair = lax.psum(partial_sums, 'rep')  19.8 us
    all_to_all x1, starting transfers between devices, per_device(): lax.all_to_all(split_keys, ('rep', 'own'), split_axis=0, concat_axis=0, t...  7.33 us
    gather x3, local copies, waits for them, and re-layouts, per_device(): block_keys = jnp.where(valid, jnp.take(padded_keys, positions, axis=0), -1)  6.28 us
    all_to_all x1, starting transfers between devices, per_device(): lax.all_to_all(split_rows, ('rep', 'own'), split_axis=0, concat_axis=0, t...  5.84 us
    gather x1, local copies, waits for them, and re-layouts, per_device(): jnp.take(padded_values, positions, axis=0)  5 us
    unnamed x14, local copies, waits for them, and re-layouts  4.68 us
  transfers between devices with their start and end apart: 5, of which 2 were waited for; matrix products, arithmetic and copies ran while one was open for 32% of the time, Pallas kernels for 0%

commit v1 on v0

--- a/solution.py
+++ b/solution.py
@@ -6,6 +6,11 @@
 
 KEYS_DEV = 4096
 CAP = 64
+
+
+def put_packet_by_axis(target):
+    local_now = jax.lax.all_gather(target, "rep").sum(axis=0)
+    return local_now
 
 
 def key_sums(rows_in, row_keys, targets):
@@ -66,7 +71,7 @@
     )
     light_sums = lax.all_gather(owned_half, "rep", axis=0, tiled=True)
     partial_sums = key_sums(values, key_ids, heavy_ids)
-    summed_pair = lax.psum(partial_sums, "rep")
+    summed_pair = put_packet_by_axis(partial_sums)
     heavy_sums = lax.psum_scatter(summed_pair, "own", scatter_dimension=0, tiled=True)
     return (light_sums, heavy_sums)
 

time: 167 us -> 217 us (1.30)
  waiting for transfers between devices: 69.9 us -> 120 us
  other arithmetic: 3.39 us -> 6.2 us
    all_gather x1, waiting for transfers between devices: 0.02 us -> 32.4 us  [per_device(): light_sums = lax.all_gather(owned_half, 'rep', axis=0, tiled=True)]
    all_gather x0 -> x1, waiting for transfers between devices: none -> 25.5 us  [put_packet_by_axis(): local_now = jax.lax.all_gather(target, 'rep').sum(axis=0)]
    psum x1 -> x0, waiting for transfers between devices: 19.8 us -> none  [per_device(): summed_pair = lax.psum(partial_sums, 'rep')]
    reduce_scatter x1, waiting for transfers between devices: 50 us -> 61.8 us  [per_device(): lax.psum_scatter(summed_pair, 'own', scatter_dimension=0, tiled=True)]
    reduce_sum x0 -> x1, other arithmetic: none -> 2.8 us  [put_packet_by_axis(): local_now = jax.lax.all_gather(target, 'rep').sum(axis=0)]
    unnamed x14 -> x11, local copies, waits for them, and re-layouts: 4.68 us -> 4.01 us
  transfers between devices with their start and end apart: 5 -> 5, of which waited for: 2 -> 3; matrix products, arithmetic and copies ran while one was open for 32% -> 26% of each run, Pallas kernels for 0% -> 0%
where the time goes in v1:
time: 217 us; the launch traced here: 216 us
  waiting for transfers between devices  120 us (55%)
  matrix products  42.9 us (20%)
  local copies, waits for them, and re-layouts  20 us (9%)
  between operations  13.9 us (6%)
  starting transfers between devices  13.5 us (6%)
  other arithmetic  6.2 us (3%)
    reduce_scatter x1, waiting for transfers between devices, per_device(): lax.psum_scatter(summed_pair, 'own', scatter_dimension=0, tiled=True)  61.8 us
    dot_general x5, matrix products, accumulate(): jnp.dot(onehot, rows_piece, precision=lax.Precision.HIGHEST, preferred_el...  42.9 us
    all_gather x1, waiting for transfers between devices, per_device(): light_sums = lax.all_gather(owned_half, 'rep', axis=0, tiled=True)  32.4 us
    all_gather x1, waiting for transfers between devices, put_packet_by_axis(): local_now = jax.lax.all_gather(target, 'rep').sum(axis=0)  25.5 us
    all_to_all x1, starting transfers between devices, per_device(): lax.all_to_all(split_keys, ('rep', 'own'), split_axis=0, concat_axis=0, t...  7.33 us
    gather x3, local copies, waits for them, and re-layouts, per_device(): block_keys = jnp.where(valid, jnp.take(padded_keys, positions, axis=0), -1)  6.28 us
    all_to_all x1, starting transfers between devices, per_device(): lax.all_to_all(split_rows, ('rep', 'own'), split_axis=0, concat_axis=0, t...  5.84 us
    gather x1, local copies, waits for them, and re-layouts, per_device(): jnp.take(padded_values, positions, axis=0)  5 us
  transfers between devices with their start and end apart: 5, of which 3 were waited for; matrix products, arithmetic and copies ran while one was open for 26% of the time, Pallas kernels for 0%

profile of v1, /device:TPU:0, one launch (start us, length us, event | category | flops | bytes accessed | tf_op | source)
XLA Modules:
  0.0 216.3 jit_solution(12231707512945634601)
XLA Ops:
  7.2 0.7 compare_select_fusion.2
  7.9 0.1 reshape.548
  8.0 0.8 concatenate.6
  8.7 0.0 copy-start.2
  8.7 0.0 copy-start.3
  8.8 6.1 %gather_fusion = s32[1024]{0:T(1024)S(1)} fusion(s32[8256]{0:T(1024)S(1)} %concatenate.6, s32[1024]{0:T(1024)S(1)} %broadcast_clamp_fusion), kind=kCustom, calls=%fused_computation | custom fusion | bytes 12288 | tf_op jit(solution)/shard_map/jit(_take)/gather | solution.py:49
  14.9 0.1 gather.13
  15.0 0.0 copy-done.2
  15.0 0.0 copy-done.3
  15.0 0.1 compare_select_fusion.5
  15.1 0.6 pad_add_fusion
  15.7 7.3 %all-to-all-start = ((s32[32,1,64]{2,1,0:T(1,128)}), s32[32,1,64]{2,1,0:T(1,128)S(1)}, u32[]{:S(2)}, u32[]{:S(2)}) async-start(s32[32,1,64]{2,1,0:T(1,128)} %bitcast.2), calls=%async_computation | async-start | bytes 32768 | tf_op jit(solution)/shard_map/all_to_all | solution.py:64
  23.0 0.1 reshape.547
  23.1 0.1 broadcast_compare_fusion.1
  23.2 3.7 %concatenate.7 = f32[8256,128]{1,0:T(8,128)} pad(f32[8192,128]{1,0:T(8,128)} %param.7, f32[]{:T(128)} %constant.82.clone.1), padding=0_64x0_0 | pad | bytes 8421380 | tf_op jit(solution)/shard_map/concatenate | solution.py:43
  26.9 0.0 copy-start.1
  26.9 0.0 copy-start.4
  26.9 5.0 %gather_fusion.1 = f32[1024,128]{1,0:T(8,128)S(1)} fusion(f32[8256,128]{1,0:T(8,128)} %concatenate.7, s32[1024]{0:T(1024)S(1)} %broadcast_clamp_fusion), kind=kCustom, calls=%fused_computation.1 | custom fusion | bytes 1052672 | tf_op jit(solution)/shard_map/jit(_take)/gather | solution.py:48
  31.9 0.7 fusion.13
  32.6 1.1 pad_maximum_fusion
  33.7 0.0 copy-done.1
  33.8 0.0 all-to-all-done
  33.8 5.8 %all-to-all-start.1 = ((f32[32,64,128]{2,1,0:T(8,128)}), f32[32,64,128]{2,1,0:T(8,128)S(1)}, u32[]{:S(2)}, u32[]{:S(2)}) async-start(f32[32,64,128]{2,1,0:T(8,128)} %bitcast.4), calls=%async_computation.1 | async-start | bytes 2097152 | tf_op jit(solution)/shard_map/all_to_all | solution.py:63
  39.6 0.0 all-gather.6.cloned.1.call-start
  39.7 0.0 copy-done.4
  39.7 34.5 %while.3 = (s32[]{:T(128)}, f32[2048,128]{1,0:T(8,128)S(1)}, s32[2048]{0:T(1024)S(1)}, s32[4,2048]{1,0:T(4,128)S(1)}, f32[4,2048,128]{2,1,0:T(8,128)}, /*index=5*/s32[]{:T(128)}, s32[]{:T(128)}) while((s32[]{:T(128)}, f32[2048,128]{1,0:T(8,128)S(1)}, s32[2048]{0:T(1024)S(1)}, s32[4,2048]{1,0:T(4,128)S(1)}, ...), condition=%wide.region_1.2_spmd.clone, body=%wide.region_0.1_spmd.clone.sunk | while | flops 6447169536 | bytes 3178599 | solution.py:32
  39.7 8.6 %fusion.34 = f32[2048,128]{1,0:T(8,128)S(1)} fusion(s32[2048]{0:T(1024)S(1)} %bitcast.23, s32[2048]{0:T(1024)S(1)} %get-tuple-element.128, f32[2048,128]{1,0:T(8,128)S(1)} %get-tuple-element.120, f32[4,2048,128]{2,1,0:T(8,128)} %get-tuple-element.130, s32[]{:T(128)S(6)} %copy.9, pred[]{:T(512)S(6)} %compare.29), kind=kOutput, calls=%fused_computation.6.clone.1 | convolution fusion | flops 6447169536 | bytes 3162117 | tf_op jit(solution)/shard_map/while/body/eval_jaxpr/dot_general | solution.py:26
  48.3 8.6 %fusion.34 = f32[2048,128]{1,0:T(8,128)S(1)} fusion(s32[2048]{0:T(1024)S(1)} %bitcast.23, s32[2048]{0:T(1024)S(1)} %get-tuple-element.128, f32[2048,128]{1,0:T(8,128)S(1)} %get-tuple-element.120, f32[4,2048,128]{2,1,0:T(8,128)} %get-tuple-element.130, s32[]{:T(128)S(6)} %copy.9, pred[]{:T(512)S(6)} %compare.29), kind=kOutput, calls=%fused_computation.6.clone.1 | convolution fusion | flops 6447169536 | bytes 3162117 | tf_op jit(solution)/shard_map/while/body/eval_jaxpr/dot_general | solution.py:26
  57.0 8.6 %fusion.34 = f32[2048,128]{1,0:T(8,128)S(1)} fusion(s32[2048]{0:T(1024)S(1)} %bitcast.23, s32[2048]{0:T(1024)S(1)} %get-tuple-element.128, f32[2048,128]{1,0:T(8,128)S(1)} %get-tuple-element.120, f32[4,2048,128]{2,1,0:T(8,128)} %get-tuple-element.130, s32[]{:T(128)S(6)} %copy.9, pred[]{:T(512)S(6)} %compare.29), kind=kOutput, calls=%fused_computation.6.clone.1 | convolution fusion | flops 6447169536 | bytes 3162117 | tf_op jit(solution)/shard_map/while/body/eval_jaxpr/dot_general | solution.py:26
  65.6 8.6 %fusion.34 = f32[2048,128]{1,0:T(8,128)S(1)} fusion(s32[2048]{0:T(1024)S(1)} %bitcast.23, s32[2048]{0:T(1024)S(1)} %get-tuple-element.128, f32[2048,128]{1,0:T(8,128)S(1)} %get-tuple-element.120, f32[4,2048,128]{2,1,0:T(8,128)} %get-tuple-element.130, s32[]{:T(128)S(6)} %copy.9, pred[]{:T(512)S(6)} %compare.29), kind=kOutput, calls=%fused_computation.6.clone.1 | convolution fusion | flops 6447169536 | bytes 3162117 | tf_op jit(solution)/shard_map/while/body/eval_jaxpr/dot_general | solution.py:26
  74.2 0.0 copy-start
  74.2 1.0 copy-done
  75.1 0.0 all-gather.6.cloned.1.call-update
  75.2 0.2 all-gather.4.cloned.1.call-start
  75.4 0.1 fusion.14
  75.5 0.1 select_n.222
  75.5 0.0 all-to-all-done.1
  75.5 8.6 %fusion.10 = f32[2048,128]{1,0:T(8,128)} fusion(f32[2048,128]{1,0:T(8,128)S(1)} %bitcast.22, s32[2048]{0:T(1024)S(1)} %select_n.222), kind=kOutput, calls=%fused_computation.12 | convolution fusion | flops 6446645248 | bytes 2105344 | tf_op jit(solution)/shard_map/while/body/eval_jaxpr/dot_general | solution.py:26
  84.1 0.0 all-gather.4.cloned.1.call-update
  84.1 0.0 reduce-scatter.2.cloned.1.call-start
  84.2 25.5 %all-gather.6.cloned.1.call-done = f32[4096,128]{1,0:T(8,128)} async-done(((f32[2048,128]{1,0:T(8,128)}), f32[4096,128]{1,0:T(8,128)}) %all-gather.6.cloned.1.call-update) | async-done | bytes 2097168 | tf_op jit(solution)/shard_map/all_gather | solution.py:12
  109.6 2.8 %reduce_sum.9 = f32[2048,128]{1,0:T(8,128)} reduce(f32[2,2048,128]{2,1,0:T(8,128)} %bitcast.21, f32[]{:T(128)} %constant.82.clone.1), dimensions={0}, to_apply=%region_2.3 | reduce | flops 262144 | bytes 3145732 | tf_op jit(solution)/shard_map/reduce_sum | solution.py:12
  112.4 0.0 reduce-scatter.2.cloned.1.call-update
  112.5 32.4 %all-gather.4.cloned.1.call-done = f32[4096,128]{1,0:T(8,128)} async-done(((f32[2048,128]{1,0:T(8,128)}), f32[4096,128]{1,0:T(8,128)}) %all-gather.4.cloned.1.call-update) | async-done | bytes 2097168 | tf_op jit(solution)/shard_map/all_gather | solution.py:72
  144.9 61.8 %reduce-scatter.2.cloned.1.call-done = f32[128,128]{1,0:T(8,128)} async-done(((f32[2048,128]{1,0:T(8,128)}), f32[128,128]{1,0:T(8,128)}) %reduce-scatter.2.cloned.1.call-update) | async-done | bytes 65552 | tf_op jit(solution)/shard_map/reduce_scatter | solution.py:75
  206.7 3.0 %copy.14 = f32[4096,128]{1,0:T(8,128)} copy(f32[4096,128]{1,0:T(8,128)} %all-gather.4.cloned.1.call-done) | data formatting | bytes 4194304
  (9 shorter events, 0.1 us)
Async XLA Ops:
  8.7 6.2 %copy-start.2 = (s32[1,16]{1,0:T(1,128)S(1)}, s32[1,16]{1,0:T(1,128)}, u32[]{:S(2)}) copy-start(s32[1,16]{1,0:T(1,128)} %param.10) | copy-start | bytes 196
  8.7 6.2 %copy-start.3 = (s32[1,16]{1,0:T(1,128)S(1)}, s32[1,16]{1,0:T(1,128)}, u32[]{:S(2)}) copy-start(s32[1,16]{1,0:T(1,128)} %param.11) | copy-start | bytes 196
  15.7 18.1 %all-to-all-start = ((s32[32,1,64]{2,1,0:T(1,128)}), s32[32,1,64]{2,1,0:T(1,128)S(1)}, u32[]{:S(2)}, u32[]{:S(2)}) async-start(s32[32,1,64]{2,1,0:T(1,128)} %bitcast.2), calls=%async_computation | async-start | bytes 32768 | tf_op jit(solution)/shard_map/all_to_all | solution.py:64
  26.9 6.8 %copy-start.1 = (s32[8192]{0:T(1024)S(1)}, s32[8192]{0:T(1024)}, u32[]{:S(2)}) copy-start(s32[8192]{0:T(1024)} %param.8) | copy-start | bytes 98308
  26.9 12.8 %copy-start.4 = (s32[2048]{0:T(1024)S(1)}, s32[2048]{0:T(1024)}, u32[]{:S(2)}) copy-start(s32[2048]{0:T(1024)} %param.9) | copy-start | bytes 24580
  33.8 41.8 %all-to-all-start.1 = ((f32[32,64,128]{2,1,0:T(8,128)}), f32[32,64,128]{2,1,0:T(8,128)S(1)}, u32[]{:S(2)}, u32[]{:S(2)}) async-start(f32[32,64,128]{2,1,0:T(8,128)} %bitcast.4), calls=%async_computation.1 | async-start | bytes 2097152 | tf_op jit(solution)/shard_map/all_to_all | solution.py:63
  39.6 70.0 %all-gather.6.cloned.1.call-start = ((), (), s32[]{:S(2)}) async-start(), calls=%async_computation.5 | async-start | bytes 3145728 | tf_op jit(solution)/shard_map/all_gather | solution.py:12
  74.2 1.0 copy-start
  75.2 69.7 %all-gather.4.cloned.1.call-start = ((), (), s32[]{:S(2)}) async-start(), calls=%async_computation.3 | async-start | bytes 3145728 | tf_op jit(solution)/shard_map/all_gather | solution.py:72
  84.1 122.6 %reduce-scatter.2.cloned.1.call-start = ((), (), s32[]{:S(2)}) async-start(), calls=%async_computation.4 | async-start | bytes 1114112 | tf_op jit(solution)/shard_map/reduce_scatter | solution.py:75
Sparse Core Ops, SparseCore 0:
  75.3 34.3 all-gather.5
  111.8 33.0 all-gather.3
  149.1 57.5 reduce-scatter.1
